TPU v7x, 256 devices: a whole 4x4x8 slice. The times are simulated.
256 devices in a mesh: expert: 16 (over z, core), shard: 16 (over y, x).
Axes of the slice: x: 4, y: 4, z: 8, core: 2. Of those that a mesh axis runs over, the one named last changes fastest.
Arguments:
- w_down: float32 [64, 1024, 2048], P('expert', None, 'shard'), may hold values from -0.25 to 0.25
- avg_down: float32 [64, 1024, 2048], P('expert', None, 'shard'), may hold values from -0.1875 to 0.1875
- mix_share: float32 [64], P('expert'), may hold values from 0.2 to 0.8
- router_weight: float32 [2048, 64], P('shard', 'expert'), may hold values from -0.125 to 0.125
- router_gain: float32 [2048], P('shard'), may hold values from 0.25 to 1.75
Outputs:
- serve_down: bfloat16 [64, 1024, 2048], P('expert')
- scale_down: float32 [64, 1024], P('expert')
- serve_router: bfloat16 [2048, 64], replicated
All inputs are finite; a program needn't handle non-finite values. Where the computation divides by a largest or mean magnitude, that divisor is 1e-20 or more.
Results may differ from a plain program's by a relative error of at most 0.001.
Values may be sent and summed in bfloat16 or wider, within the bound.
No kernel may reach another device: no remote copies, remote signals or barrier semaphores. Data moves between devices by JAX's collectives and lax.ppermute only.
A program may use at most 128 MiB of HBM per device.

v0:
```python
import jax
import jax.numpy as jnp
from jax import lax
from jax.sharding import PartitionSpec as P

D_MODEL = 2048


def sent_to_all(value, axis):
    copies = jnp.broadcast_to(value, (lax.axis_size(axis), *value.shape))
    return lax.all_to_all(copies, axis, split_axis=0, concat_axis=0, tiled=True)


def taken_together(value, axis):
    everything = sent_to_all(value, axis)
    return jnp.sum(everything, axis=0)


def laid_out(tiles, dim):
    shape = list(tiles.shape[1:])
    shape[dim] *= tiles.shape[0]
    return jnp.moveaxis(tiles, 0, dim).reshape(shape)


def gathered_copies(value, axis, dim):
    return laid_out(sent_to_all(value, axis), dim)


def body(w_down, avg_down, mix_share, router_weight, router_gain):
    fresh_down = mix_share[:, None, None] * w_down + (1.0 - mix_share[:, None, None]) * avg_down
    total_down = taken_together(jnp.sum(jnp.abs(fresh_down), axis=2), "shard")
    scale_down = total_down / D_MODEL
    narrow_down = (fresh_down / jnp.expand_dims(scale_down, 2)).astype(jnp.bfloat16)
    serve_down = lax.all_gather(narrow_down, "shard", axis=2, tiled=True)
    part_router = (router_weight * router_gain[:, None]).astype(jnp.bfloat16)
    row_router = gathered_copies(part_router, "shard", 0)
    serve_router = lax.all_gather(row_router, "expert", axis=1, tiled=True)
    return (serve_down, scale_down, serve_router)


def solution(mesh):
    return jax.shard_map(
        body,
        mesh=mesh,
        in_specs=(
            P("expert", None, "shard"),
            P("expert", None, "shard"),
            P("expert"),
            P("shard", "expert"),
            P("shard"),
        ),
        out_specs=(P("expert", None, None), P("expert", None), P()),
        check_vma=False,
    )
```

profile of v0, /device:TPU:2, one launch (start us, length us, event | category | flops | bytes accessed | tf_op | source)
XLA Modules:
  0.0 174.2 jit_solution(17278753643345742411)
XLA Ops:
  7.2 0.0 all-gather.3.cloned.1.call-start
  7.2 0.7 broadcast_subtract_fusion
  7.9 0.0 copy-start
  7.9 0.0 copy-start.2
  7.9 3.1 %abs_reduce_fusion = f32[4,1024]{1,0:T(4,128)S(1)} fusion(f32[4,1024,128]{2,1,0:T(8,128)} %param.6, f32[4]{0:T(128)S(1)} %broadcast_subtract_fusion, f32[4,1024,128]{2,1,0:T(8,128)} %param.5, f32[4]{0:T(128)} %param.7), kind=kLoop, calls=%fused_computation.1 | loop fusion | flops 2617344 | bytes 4210720 | tf_op jit(solution)/shard_map/reduce_sum | solution.py:31
  11.0 14.6 %all_to_all.10 = f32[16,4,1024]{2,1,0:T(4,128)S(1)} all-to-all(f32[16,4,1024]{2,1,0:T(4,128)S(1)} %broadcast_in_dim.4), channel_id=1, replica_groups=mesh['expert'=16,'shard'=16] {'shard'}, dimensions={0} | all-to-all | bytes 524288 | tf_op jit(solution)/shard_map/all_to_all | solution.py:11
  25.6 0.1 reduce_sum.19
  25.7 0.0 copy-done
  25.7 0.0 copy-done.2
  25.7 0.0 copy-start.1
  25.7 0.0 copy-start.3
  25.7 0.0 copy-start.4
  25.7 2.8 %divide_convert_fusion = bf16[4,1024,128]{2,1,0:T(8,128)(2,1)} fusion(f32[4,1024]{1,0:T(4,128)S(1)} %broadcast_multiply_fusion, f32[4,1024,128]{2,1,0:T(8,128)S(1)} %copy-done, f32[4]{0:T(128)S(1)} %broadcast_subtract_fusion, f32[4,1024,128]{2,1,0:T(8,128)} %param.5, f32[4]{0:T(128)S(1)} %copy-done.2), kind=kLoop, calls=%fused_computation | loop fusion | flops 2621440 | bytes 5259296 | tf_op jit(solution)/shard_map/convert_element_type | solution.py:33
  28.5 0.0 copy-done.1
  28.5 0.0 all-gather.3.cloned.1.call-update
  28.5 0.0 copy-done.3
  28.5 0.0 copy-done.4
  28.6 10.5 %all_to_all.11 = bf16[16,128,4]{1,2,0:T(4,128)(2,1)S(1)} all-to-all(bf16[16,128,4]{1,2,0:T(4,128)(2,1)S(1)} %broadcast_in_dim.5), channel_id=1, replica_groups=mesh['expert'=16,'shard'=16] {'shard'}, dimensions={0} | all-to-all | bytes 32768 | tf_op jit(solution)/shard_map/all_to_all | solution.py:11
  39.1 20.7 %all-gather = bf16[16,4,2048]{2,1,0:T(4,128)(2,1)S(1)} all-gather(bf16[1,4,2048]{2,1,0:T(4,128)(2,1)S(1)} %bitcast.7), channel_id=1, replica_groups=mesh['expert'=16,'shard'=16] {'expert'}, dimensions={0}, use_global_device_ids=true | all-gather | bytes 278528 | tf_op jit(solution)/shard_map/all_gather | solution.py:37
  59.7 0.8 reshape.18
  60.5 92.7 %all-gather.3.cloned.1.call-done = bf16[4,1024,2048]{2,1,0:T(8,128)(2,1)} async-done(((bf16[4,1024,128]{2,1,0:T(8,128)(2,1)}), bf16[4,1024,2048]{2,1,0:T(8,128)(2,1)}) %all-gather.3.cloned.1.call-update) | async-done | bytes 16777232 | tf_op jit(solution)/shard_map/all_gather | solution.py:34
  153.2 14.2 %copy.11 = bf16[4,1024,2048]{2,1,0:T(8,128)(2,1)} copy(bf16[4,1024,2048]{2,1,0:T(8,128)(2,1)} %all-gather.3.cloned.1.call-done) | data formatting | bytes 33554432
  (4 shorter events, 0.1 us)
Async XLA Ops:
  7.2 146.0 %all-gather.3.cloned.1.call-start = ((), (), s32[]{:S(2)}) async-start(), calls=%async_computation.2 | async-start | bytes 17825792 | tf_op jit(solution)/shard_map/all_gather | solution.py:34
  7.9 17.8 %copy-start = (f32[4,1024,128]{2,1,0:T(8,128)S(1)}, f32[4,1024,128]{2,1,0:T(8,128)}, u32[]{:S(2)}) copy-start(f32[4,1024,128]{2,1,0:T(8,128)} %param.6) | copy-start | bytes 6291460
  7.9 17.8 %copy-start.2 = (f32[4]{0:T(128)S(1)}, f32[4]{0:T(128)}, u32[]{:S(2)}) copy-start(f32[4]{0:T(128)} %param.7) | copy-start | bytes 52
  25.7 2.8 %copy-start.1 = (f32[4,1024]{1,0:T(4,128)}, f32[4,1024]{1,0:T(4,128)S(1)}, u32[]{:S(2)}) copy-start(f32[4,1024]{1,0:T(4,128)S(1)} %broadcast_multiply_fusion) | copy-start | bytes 49156
  25.7 2.8 %copy-start.3 = (f32[128,4]{0,1:T(4,128)S(1)}, f32[128,4]{0,1:T(4,128)}, u32[]{:S(2)}) copy-start(f32[128,4]{0,1:T(4,128)} %param.8) | copy-start | bytes 6148
  25.7 2.8 %copy-start.4 = (f32[128]{0:T(128)S(1)}, f32[128]{0:T(128)}, u32[]{:S(2)}) copy-start(f32[128]{0:T(128)} %param.9) | copy-start | bytes 1540
Sparse Core Ops, SparseCore 0:
  28.6 124.4 all-gather.2
where the time goes:
time: 174 us
  waiting for transfers between devices  92.7 us (53%)
  blocking collectives  45.8 us (26%)
  local copies, waits for them, and re-layouts  15 us (9%)
  between operations  14.1 us (8%)
  other arithmetic  6.58 us (4%)
    all_gather x1, waiting for transfers between devices, body(): serve_down = lax.all_gather(narrow_down, 'shard', axis=2, tiled=True)  92.7 us
    all_to_all x2, blocking collectives, sent_to_all(): return lax.all_to_all(copies, axis, split_axis=0, concat_axis=0, tiled=True)  25.1 us
    all_gather x1, blocking collectives, body(): serve_router = lax.all_gather(row_router, 'expert', axis=1, tiled=True)  20.7 us
    unnamed x12, local copies, waits for them, and re-layouts  14.9 us
  transfers between devices with their start and end apart: 1, of which 1 were waited for; matrix products, arithmetic and copies ran while one was open for 0% of the time, Pallas kernels for 0%

commit v1 on v0

--- a/solution.py
+++ b/solution.py
@@ -31,7 +31,11 @@
     total_down = taken_together(jnp.sum(jnp.abs(fresh_down), axis=2), "shard")
     scale_down = total_down / D_MODEL
     narrow_down = (fresh_down / jnp.expand_dims(scale_down, 2)).astype(jnp.bfloat16)
-    serve_down = lax.all_gather(narrow_down, "shard", axis=2, tiled=True)
+    n_peers_all = jax.lax.axis_size("shard")
+    made = [n_peers_all if ix == 2 else 1 for ix in range(narrow_down.ndim)]
+    serve_down = jax.lax.all_to_all(
+        jnp.tile(narrow_down, made), "shard", split_axis=2, tiled=True, concat_axis=2
+    )
     part_router = (router_weight * router_gain[:, None]).astype(jnp.bfloat16)
     row_router = gathered_copies(part_router, "shard", 0)
     serve_router = lax.all_gather(row_router, "expert", axis=1, tiled=True)

time: 174 us -> 315 us (1.81); the launches traced: 174 us -> 311 us
  waiting for transfers between devices: 92.7 us -> 228 us
  blocking collectives: 45.8 us -> 20.7 us
  local copies, waits for them, and re-layouts: 15 us -> 36.8 us
  starting transfers between devices: 0.04 us -> 18.5 us
  between operations: 14.1 us -> 0.71 us
    all_to_all x0 -> x3, waiting for transfers between devices: none -> 228 us  [the longest x1 218 us: body(): jax.lax.all_to_all(jnp.tile(narrow_down, made), 'shard', split_axis=2, ti...]
    all_gather x1 -> x0, waiting for transfers between devices: 92.7 us -> none  [body(): serve_down = lax.all_gather(narrow_down, 'shard', axis=2, tiled=True)]
    all_to_all x2 -> x0, blocking collectives: 25.1 us -> none  [sent_to_all(): return lax.all_to_all(copies, axis, split_axis=0, concat_axis=0, tiled=True)]
    all_to_all x0 -> x3, starting transfers between devices: none -> 18.5 us  [the longest x2 12.2 us: sent_to_all(): return lax.all_to_all(copies, axis, split_axis=0, concat_axis=0, tiled=True)]
    unnamed x12, local copies, waits for them, and re-layouts: 14.9 us -> 26.8 us
    another operation x0 -> x1, local copies, waits for them, and re-layouts: none -> 7.66 us  [body(): jnp.tile(narrow_down, made)]
  transfers between devices with their start and end apart: 1 -> 3, of which waited for: 1 -> 3; matrix products, arithmetic and copies ran while one was open for 0% -> 1% of each run, Pallas kernels for 0% -> 0%
where the time goes in v1:
time: 315 us; the launch traced here: 311 us
  waiting for transfers between devices  228 us (72%)
  local copies, waits for them, and re-layouts  36.8 us (12%)
  blocking collectives  20.7 us (7%)
  starting transfers between devices  18.5 us (6%)
  other arithmetic  5.8 us (2%)
    all_to_all x1, waiting for transfers between devices, body(): jax.lax.all_to_all(jnp.tile(narrow_down, made), 'shard', split_axis=2, ti...  218 us
    unnamed x12, local copies, waits for them, and re-layouts  26.8 us
    all_gather x1, blocking collectives, body(): serve_router = lax.all_gather(row_router, 'expert', axis=1, tiled=True)  20.7 us
    all_to_all x2, starting transfers between devices, sent_to_all(): return lax.all_to_all(copies, axis, split_axis=0, concat_axis=0, tiled=True)  12.2 us
    all_to_all x2, waiting for transfers between devices, sent_to_all(): return lax.all_to_all(copies, axis, split_axis=0, concat_axis=0, tiled=True)  10.6 us
    another operation x1, local copies, waits for them, and re-layouts, body(): jnp.tile(narrow_down, made)  7.66 us
    all_to_all x1, starting transfers between devices, body(): jax.lax.all_to_all(jnp.tile(narrow_down, made), 'shard', split_axis=2, ti...  6.32 us
  transfers between devices with their start and end apart: 3, of which 3 were waited for; matrix products, arithmetic and copies ran while one was open for 1% of the time, Pallas kernels for 0%

profile of v1, /device:TPU:2, one launch (start us, length us, event | category | flops | bytes accessed | tf_op | source)
XLA Modules:
  0.0 310.9 jit_solution(11970901923644132086)
XLA Ops:
  0.6 0.7 broadcast_subtract_fusion
  1.3 0.0 copy-start.3
  1.3 3.1 abs_reduce_fusion
  4.4 0.8 broadcast_in_dim.4
  5.1 7.5 %all-to-all-start = ((f32[16,4,1024]{2,1,0:T(4,128)}), f32[16,4,1024]{2,1,0:T(4,128)S(1)}, u32[]{:S(2)}, u32[]{:S(2)}) async-start(f32[16,4,1024]{2,1,0:T(4,128)} %broadcast_in_dim.4), calls=%async_computation | async-start | bytes 524288 | tf_op jit(solution)/shard_map/all_to_all | solution.py:11
  12.6 0.0 copy-done.3
  12.6 0.0 copy-done.4
  12.6 7.3 %all-to-all-done = f32[16,4,1024]{2,1,0:T(4,128)S(1)} async-done(((f32[16,4,1024]{2,1,0:T(4,128)}), f32[16,4,1024]{2,1,0:T(4,128)S(1)}, u32[]{:S(2)}, u32[]{:S(2)}) %all-to-all-start) | async-done | bytes 262176 | tf_op jit(solution)/shard_map/all_to_all | solution.py:11
  20.0 0.6 broadcast_in_dim.5
  20.6 4.7 %all-to-all-start.2 = ((bf16[16,128,4]{1,2,0:T(4,128)(2,1)}), bf16[16,128,4]{1,2,0:T(4,128)(2,1)S(1)}, u32[]{:S(2)}, u32[]{:S(2)}) async-start(bf16[16,128,4]{1,2,0:T(4,128)(2,1)} %broadcast_in_dim.5), calls=%async_computation.2 | async-start | bytes 32768 | tf_op jit(solution)/shard_map/all_to_all | solution.py:11
  25.3 0.1 reduce_sum.19
  25.4 0.0 copy-done
  25.4 0.0 copy-done.2
  25.4 0.0 copy-start.1
  25.4 2.0 divide_convert_fusion
  27.4 0.0 copy-done.1
  27.4 0.9 copy.13
  28.3 3.3 %all-to-all-done.2 = bf16[16,128,4]{1,2,0:T(4,128)(2,1)S(1)} async-done(((bf16[16,128,4]{1,2,0:T(4,128)(2,1)}), bf16[16,128,4]{1,2,0:T(4,128)(2,1)S(1)}, u32[]{:S(2)}, u32[]{:S(2)}) %all-to-all-start.2) | async-done | bytes 16416 | tf_op jit(solution)/shard_map/all_to_all | solution.py:11
  31.6 7.7 %tile.4 = bf16[4,1024,16,128]{1,0,3,2:T(4,128)(2,1)} broadcast(bf16[4,1024,128]{1,0,2:T(4,128)(2,1)S(1)} %copy.13), dimensions={0,1,3} | broadcast | bytes 17825792 | tf_op jit(solution)/shard_map/tile | solution.py:37
  39.3 6.3 %all-to-all-start.1 = ((bf16[4,1024,2048]{1,0,2:T(4,128)(2,1)}), bf16[4,1024,2048]{1,0,2:T(4,128)(2,1)}, u32[]{:S(2)}, u32[]{:S(2)}) async-start(bf16[4,1024,2048]{1,0,2:T(4,128)(2,1)} %bitcast.7), calls=%async_computation.1 | async-start | bytes 33554432 | tf_op jit(solution)/shard_map/all_to_all | solution.py:36
  45.6 20.7 %all-gather = bf16[16,4,2048]{2,1,0:T(4,128)(2,1)S(1)} all-gather(bf16[1,4,2048]{2,1,0:T(4,128)(2,1)S(1)} %bitcast.9), channel_id=1, replica_groups=mesh['expert'=16,'shard'=16] {'expert'}, dimensions={0}, use_global_device_ids=true | all-gather | bytes 278528 | tf_op jit(solution)/shard_map/all_gather | solution.py:41
  66.2 0.8 reshape.22
  67.0 217.9 %all-to-all-done.1 = bf16[4,1024,2048]{1,0,2:T(4,128)(2,1)} async-done(((bf16[4,1024,2048]{1,0,2:T(4,128)(2,1)}), bf16[4,1024,2048]{1,0,2:T(4,128)(2,1)}, u32[]{:S(2)}, u32[]{:S(2)}) %all-to-all-start.1) | async-done | bytes 16777248 | tf_op jit(solution)/shard_map/all_to_all | solution.py:36
  284.9 26.0 %copy.14 = bf16[4,1024,2048]{2,1,0:T(8,128)(2,1)} copy(bf16[4,1024,2048]{1,0,2:T(4,128)(2,1)} %all-to-all-done.1) | data formatting | bytes 33554432
  (5 shorter events, 0.0 us)
Async XLA Ops:
  1.3 11.3 %copy-start.3 = (f32[128,4]{0,1:T(4,128)S(1)}, f32[128,4]{0,1:T(4,128)}, u32[]{:S(2)}) copy-start(f32[128,4]{0,1:T(4,128)} %param.8) | copy-start | bytes 6148
  1.3 11.3 %copy-start.4 = (f32[128]{0:T(128)S(1)}, f32[128]{0:T(128)}, u32[]{:S(2)}) copy-start(f32[128]{0:T(128)} %param.9) | copy-start | bytes 1540
  1.3 24.1 %copy-start = (f32[4,1024,128]{2,1,0:T(8,128)S(1)}, f32[4,1024,128]{2,1,0:T(8,128)}, u32[]{:S(2)}) copy-start(f32[4,1024,128]{2,1,0:T(8,128)} %param.6) | copy-start | bytes 6291460
  1.3 24.1 %copy-start.2 = (f32[4]{0:T(128)S(1)}, f32[4]{0:T(128)}, u32[]{:S(2)}) copy-start(f32[4]{0:T(128)} %param.7) | copy-start | bytes 52
  5.1 14.8 %all-to-all-start = ((f32[16,4,1024]{2,1,0:T(4,128)}), f32[16,4,1024]{2,1,0:T(4,128)S(1)}, u32[]{:S(2)}, u32[]{:S(2)}) async-start(f32[16,4,1024]{2,1,0:T(4,128)} %broadcast_in_dim.4), calls=%async_computation | async-start | bytes 524288 | tf_op jit(solution)/shard_map/all_to_all | solution.py:11
  20.6 11.0 %all-to-all-start.2 = ((bf16[16,128,4]{1,2,0:T(4,128)(2,1)}), bf16[16,128,4]{1,2,0:T(4,128)(2,1)S(1)}, u32[]{:S(2)}, u32[]{:S(2)}) async-start(bf16[16,128,4]{1,2,0:T(4,128)(2,1)} %broadcast_in_dim.5), calls=%async_computation.2 | async-start | bytes 32768 | tf_op jit(solution)/shard_map/all_to_all | solution.py:11
  25.4 2.0 copy-start.1
  39.3 245.6 %all-to-all-start.1 = ((bf16[4,1024,2048]{1,0,2:T(4,128)(2,1)}), bf16[4,1024,2048]{1,0,2:T(4,128)(2,1)}, u32[]{:S(2)}, u32[]{:S(2)}) async-start(bf16[4,1024,2048]{1,0,2:T(4,128)(2,1)} %bitcast.7), calls=%async_computation.1 | async-start | bytes 33554432 | tf_op jit(solution)/shard_map/all_to_all | solution.py:36
